TPU v7x, 256 devices: a whole 4x4x8 slice. The times are simulated.
256 devices in a mesh: head: 8 (over z_hi, core), outer: 2 (over z_lo), inner: 16 (over y, x).
Axes of the slice: x: 4, y: 4, z: 8 (z_hi: 4, z_lo: 2; z = z_hi * 2 + z_lo), core: 2. Of those that a mesh axis runs over, the one named last changes fastest.
Arguments:
- query: bfloat16 [32768, 8192], P(('outer', 'inner', 'head')), may hold values from -100 to 100
- keys: bfloat16 [32768, 1024], P(('outer', 'inner', 'head')), may hold values from -4.5 to 4.5
- values: bfloat16 [32768, 1024], P(('outer', 'inner', 'head')), may hold values from -6 to 6
- lengths: int32 [32], replicated, may hold values from 1 to 2048, 32768 in all
Outputs:
- attended: bfloat16 [32768, 8192], P(('outer', 'inner', 'head'))
Inputs may be any that keep to these rules, and one draw needn't show every extreme that they name: `lengths`: they sum to 32768, and the longest is exactly 2048.
All inputs are finite; a program needn't handle non-finite values.
Results may differ from a plain program's by a relative error of at most 0.0038.
Values may be sent and summed in bfloat16 or wider, within the bound.
A program may use at most 64 MiB of HBM per device.

v0:
```python
import math

import jax
import jax.numpy as jnp
from jax import lax
from jax.sharding import PartitionSpec as P

HEAD_SIZE = 128


def from_behind(value, axis, steps):
    count = lax.axis_size(axis)
    leading, last = (max(0, -steps), min(count, count - steps))
    return lax.ppermute(value, axis, [(source, source + steps) for source in range(leading, last)])


def doc_numbers(lengths, start_pos, count):
    ends = jnp.cumsum(lengths)
    positions = start_pos + lax.iota(jnp.int32, count)
    numbers = jnp.sum((positions[:, None] >= ends[None, :]).astype(jnp.int32), axis=1)
    return (numbers, positions)


def per_device(query, keys, values, lengths):
    query_local, keys_local, values_local = (
        lax.all_to_all(query, "head", split_axis=1, concat_axis=0, tiled=True),
        lax.all_to_all(keys, "head", split_axis=1, concat_axis=0, tiled=True),
        lax.all_to_all(values, "head", split_axis=1, concat_axis=0, tiled=True),
    )
    local_len = query_local.shape[0]
    pair_heads = keys_local.shape[1] // HEAD_SIZE
    group_width = query_local.shape[1] // keys_local.shape[1]
    context_count = lax.axis_size(("outer", "inner"))
    reach_hops = min(2, context_count // 4)
    position_index = lax.axis_index(("outer", "inner"))
    query_docs, query_pos = doc_numbers(lengths, position_index * local_len, local_len)
    query_groups = jnp.transpose(
        query_local.reshape(local_len, pair_heads, group_width, HEAD_SIZE), (2, 0, 1, 3)
    )
    score_scale = 1.0 / math.sqrt(HEAD_SIZE)

    def attend(state, stacked, distance):
        key_heads = stacked[0].reshape(local_len, pair_heads, HEAD_SIZE)
        value_heads = stacked[1].reshape(local_len, pair_heads, HEAD_SIZE)
        key_docs, key_pos = doc_numbers(lengths, (position_index - distance) * local_len, local_len)
        visible = (
            (query_docs[:, None] == key_docs[None, :])
            & (key_pos[None, :] <= query_pos[:, None])
            & (key_pos[None, :] >= 0)
        )

        def one_group(operands):
            query_part, running_max, running_total, running_sum = operands
            scores = (
                jnp.einsum(
                    "qkd,ckd->kqc", query_part, key_heads, preferred_element_type=jnp.float32
                )
                * score_scale
            )
            masked = jnp.where(visible, scores, -1e30)
            new_max = jnp.maximum(running_max, jnp.max(masked, axis=2))
            weights = jnp.where(visible, jnp.exp(masked - new_max[..., None]), 0.0)
            shrink = jnp.exp(running_max - new_max)
            new_total = running_total * shrink + jnp.sum(weights, axis=2)
            update = jnp.einsum(
                "kqc,ckd->qkd",
                weights.astype(jnp.bfloat16),
                value_heads,
                preferred_element_type=jnp.float32,
            )
            new_sum = running_sum * jnp.transpose(shrink, (1, 0))[..., None] + update
            return (new_max, new_total, new_sum)

        return lax.map(one_group, (query_groups, state[0], state[1], state[2]))

    start_state = (
        jnp.full((group_width, pair_heads, local_len), -1e30, jnp.float32),
        jnp.zeros((group_width, pair_heads, local_len), jnp.float32),
        jnp.zeros((group_width, local_len, pair_heads, HEAD_SIZE), jnp.float32),
    )
    own_pair = jnp.stack((keys_local, values_local))
    state = attend(start_state, own_pair, 0)
    carried = own_pair
    for distance in range(1, reach_hops + 1):
        carried = from_behind(carried, ("outer", "inner"), 1)
        state = attend(state, carried, distance)
    running_max, running_total, running_sum = state
    outcome = running_sum / jnp.transpose(running_total, (0, 2, 1))[..., None]
    outcome = jnp.transpose(outcome, (1, 2, 0, 3))
    outcome = outcome.reshape(local_len, pair_heads * group_width * HEAD_SIZE).astype(jnp.bfloat16)
    return lax.all_to_all(outcome, "head", split_axis=0, concat_axis=1, tiled=True)


def solution(mesh):
    placed = (
        P(("outer", "inner", "head"), None),
        P(("outer", "inner", "head"), None),
        P(("outer", "inner", "head"), None),
        P(),
    )
    return jax.shard_map(
        per_device,
        mesh=mesh,
        in_specs=placed,
        out_specs=P(("outer", "inner", "head"), None),
        check_vma=False,
    )
```

profile of v0, /device:TPU:32, one launch (start us, length us, event | category | flops | bytes accessed | tf_op | source)
XLA Modules:
  0.0 370.6 jit_solution(17014296130180950947)
XLA Ops:
  1.8 7.6 %all-to-all-start.1 = ((bf16[128,8,128]{0,2,1:T(8,128)(2,1)}), bf16[128,8,128]{0,2,1:T(8,128)(2,1)S(1)}, u32[]{:S(2)}, u32[]{:S(2)}) async-start(bf16[128,8,128]{0,2,1:T(8,128)(2,1)} %bitcast.2), calls=%async_computation.1 | async-start | bytes 524288 | tf_op jit(solution)/shard_map/all_to_all | solution.py:27
  11.1 9.2 %all-to-all-done.1 = bf16[128,8,128]{0,2,1:T(8,128)(2,1)S(1)} async-done(((bf16[128,8,128]{0,2,1:T(8,128)(2,1)}), bf16[128,8,128]{0,2,1:T(8,128)(2,1)S(1)}, u32[]{:S(2)}, u32[]{:S(2)}) %all-to-all-start.1) | async-done | bytes 262176 | tf_op jit(solution)/shard_map/all_to_all | solution.py:27
  20.3 3.6 all-to-all-start.2
  23.9 3.1 copy.62
  27.1 9.6 %all-to-all-done.2 = bf16[128,8,128]{0,2,1:T(8,128)(2,1)S(1)} async-done(((bf16[128,8,128]{0,2,1:T(8,128)(2,1)}), bf16[128,8,128]{0,2,1:T(8,128)(2,1)S(1)}, u32[]{:S(2)}, u32[]{:S(2)}) %all-to-all-start.2) | async-done | bytes 262176 | tf_op jit(solution)/shard_map/all_to_all | solution.py:28
  36.6 3.6 all-to-all-start
  41.5 3.4 collective-permute-start
  44.9 58.5 %collective-permute-done = bf16[2,1024,128]{2,1,0:T(8,128)(2,1)} collective-permute-done((bf16[2,1024,128]{2,1,0:T(8,128)(2,1)}, bf16[2,1024,128]{2,1,0:T(8,128)(2,1)}, u32[]{:S(2)}, u32[]{:S(2)}) %collective-permute-start) | collective-permute-done | bytes 524320 | tf_op jit(solution)/shard_map/ppermute | solution.py:14
  107.7 15.8 %collective-permute-done.1 = bf16[2,1024,128]{2,1,0:T(8,128)(2,1)} collective-permute-done((bf16[2,1024,128]{2,1,0:T(8,128)(2,1)}, bf16[2,1024,128]{2,1,0:T(8,128)(2,1)}, u32[]{:S(2)}, u32[]{:S(2)}) %collective-permute-start.1) | collective-permute-done | bytes 524320 | tf_op jit(solution)/shard_map/ppermute | solution.py:14
  127.9 53.4 %while.43 = (s32[]{:T(128)}, f32[8,1,1024]{2,1,0:T(1,128)S(1)}, f32[8,1,1024]{2,1,0:T(1,128)S(1)}, f32[8,1024,1,128]{3,1,2,0:T(8,128)}, bf16[8,1024,1,128]{3,1,2...) while((s32[]{:T(128)}, f32[8,1,1024]{2,1,0:T(1,128)S(1)}, ...), condition=%wide.region_5.6_spmd.clone, body=%wide.region_2.0_spmd.clone.sunk | while | flops 563220480 | bytes 13987445 | solution.py:74
  136.1 3.0 fusion.106
  162.8 3.0 fusion.106
  183.7 61.7 %while.44 = (s32[]{:T(128)}, f32[8,1,1024]{2,1,0:T(1,128)S(1)}, f32[8,1,1024]{2,1,0:T(1,128)S(1)}, f32[8,1024,1,128]{3,1,2,0:T(8,128)}, f32[8,1,1024]{2,1,0:T(1,...) while((s32[]{:T(128)}, f32[8,1,1024]{2,1,0:T(1,128)S(1)}, ...), condition=%wide.region_10.11_spmd.clone, body=%wide.region_7.10_spmd.clone.sunk | while | flops 563351552 | bytes 14540449 | solution.py:74
  185.1 4.0 %fusion.111 = f32[8,1024,1,128]{3,1,2,0:T(8,128)} fusion(f32[8,1024,1,128]{3,1,2,0:T(8,128)} %get-tuple-element.859, s32[]{:T(128)} %get-tuple-element.856, f32[1024,1024]{0,1:T(8,128)S(1)} %get-tuple-element.783, f32[1024]{0:T(1024)S(1)} %get-tuple-element.785, f32[8,1024,1,128]{3,1,2,0:T(8,128)} %get-tuple-element.880, ...), kind=kOutput, calls=%fused_computation.37.clone.1 | convolution fusion | flops 278134784 | bytes 5531136 | tf_op jit(solution)/shard_map/while/body/eval_jaxpr/kqc,ckd->qkd/dot_general | solution.py:65
  192.8 4.0 %fusion.111 = f32[8,1024,1,128]{3,1,2,0:T(8,128)} fusion(f32[8,1024,1,128]{3,1,2,0:T(8,128)} %get-tuple-element.859, s32[]{:T(128)} %get-tuple-element.856, f32[1024,1024]{0,1:T(8,128)S(1)} %get-tuple-element.783, f32[1024]{0:T(1024)S(1)} %get-tuple-element.785, f32[8,1024,1,128]{3,1,2,0:T(8,128)} %get-tuple-element.880, ...), kind=kOutput, calls=%fused_computation.37.clone.1 | convolution fusion | flops 278134784 | bytes 5531136 | tf_op jit(solution)/shard_map/while/body/eval_jaxpr/kqc,ckd->qkd/dot_general | solution.py:65
  200.6 4.0 %fusion.111 = f32[8,1024,1,128]{3,1,2,0:T(8,128)} fusion(f32[8,1024,1,128]{3,1,2,0:T(8,128)} %get-tuple-element.859, s32[]{:T(128)} %get-tuple-element.856, f32[1024,1024]{0,1:T(8,128)S(1)} %get-tuple-element.783, f32[1024]{0:T(1024)S(1)} %get-tuple-element.785, f32[8,1024,1,128]{3,1,2,0:T(8,128)} %get-tuple-element.880, ...), kind=kOutput, calls=%fused_computation.37.clone.1 | convolution fusion | flops 278134784 | bytes 5531136 | tf_op jit(solution)/shard_map/while/body/eval_jaxpr/kqc,ckd->qkd/dot_general | solution.py:65
  208.3 4.0 %fusion.111 = f32[8,1024,1,128]{3,1,2,0:T(8,128)} fusion(f32[8,1024,1,128]{3,1,2,0:T(8,128)} %get-tuple-element.859, s32[]{:T(128)} %get-tuple-element.856, f32[1024,1024]{0,1:T(8,128)S(1)} %get-tuple-element.783, f32[1024]{0:T(1024)S(1)} %get-tuple-element.785, f32[8,1024,1,128]{3,1,2,0:T(8,128)} %get-tuple-element.880, ...), kind=kOutput, calls=%fused_computation.37.clone.1 | convolution fusion | flops 278134784 | bytes 5531136 | tf_op jit(solution)/shard_map/while/body/eval_jaxpr/kqc,ckd->qkd/dot_general | solution.py:65
  216.0 4.0 %fusion.111 = f32[8,1024,1,128]{3,1,2,0:T(8,128)} fusion(f32[8,1024,1,128]{3,1,2,0:T(8,128)} %get-tuple-element.859, s32[]{:T(128)} %get-tuple-element.856, f32[1024,1024]{0,1:T(8,128)S(1)} %get-tuple-element.783, f32[1024]{0:T(1024)S(1)} %get-tuple-element.785, f32[8,1024,1,128]{3,1,2,0:T(8,128)} %get-tuple-element.880, ...), kind=kOutput, calls=%fused_computation.37.clone.1 | convolution fusion | flops 278134784 | bytes 5531136 | tf_op jit(solution)/shard_map/while/body/eval_jaxpr/kqc,ckd->qkd/dot_general | solution.py:65
  223.7 4.0 %fusion.111 = f32[8,1024,1,128]{3,1,2,0:T(8,128)} fusion(f32[8,1024,1,128]{3,1,2,0:T(8,128)} %get-tuple-element.859, s32[]{:T(128)} %get-tuple-element.856, f32[1024,1024]{0,1:T(8,128)S(1)} %get-tuple-element.783, f32[1024]{0:T(1024)S(1)} %get-tuple-element.785, f32[8,1024,1,128]{3,1,2,0:T(8,128)} %get-tuple-element.880, ...), kind=kOutput, calls=%fused_computation.37.clone.1 | convolution fusion | flops 278134784 | bytes 5531136 | tf_op jit(solution)/shard_map/while/body/eval_jaxpr/kqc,ckd->qkd/dot_general | solution.py:65
  231.5 4.0 %fusion.111 = f32[8,1024,1,128]{3,1,2,0:T(8,128)} fusion(f32[8,1024,1,128]{3,1,2,0:T(8,128)} %get-tuple-element.859, s32[]{:T(128)} %get-tuple-element.856, f32[1024,1024]{0,1:T(8,128)S(1)} %get-tuple-element.783, f32[1024]{0:T(1024)S(1)} %get-tuple-element.785, f32[8,1024,1,128]{3,1,2,0:T(8,128)} %get-tuple-element.880, ...), kind=kOutput, calls=%fused_computation.37.clone.1 | convolution fusion | flops 278134784 | bytes 5531136 | tf_op jit(solution)/shard_map/while/body/eval_jaxpr/kqc,ckd->qkd/dot_general | solution.py:65
  239.2 4.0 %fusion.111 = f32[8,1024,1,128]{3,1,2,0:T(8,128)} fusion(f32[8,1024,1,128]{3,1,2,0:T(8,128)} %get-tuple-element.859, s32[]{:T(128)} %get-tuple-element.856, f32[1024,1024]{0,1:T(8,128)S(1)} %get-tuple-element.783, f32[1024]{0:T(1024)S(1)} %get-tuple-element.785, f32[8,1024,1,128]{3,1,2,0:T(8,128)} %get-tuple-element.880, ...), kind=kOutput, calls=%fused_computation.37.clone.1 | convolution fusion | flops 278134784 | bytes 5531136 | tf_op jit(solution)/shard_map/while/body/eval_jaxpr/kqc,ckd->qkd/dot_general | solution.py:65
  247.7 62.6 %while.45 = (s32[]{:T(128)}, f32[8,1,1024]{2,0,1:T(8,128)S(1)}, f32[8,1024,1,128]{3,1,2,0:T(8,128)}, f32[8,1,1024]{2,1,0:T(1,128)S(1)}, f32[8,1,1024]{2,1,0:T(1,...) while((s32[]{:T(128)}, f32[8,1,1024]{2,0,1:T(8,128)S(1)}, ...), condition=%wide.region_15.16_spmd.clone, body=%wide.region_12.15_spmd.clone.sunk | while | flops 563351552 | bytes 14544549 | solution.py:74
  249.2 4.0 %fusion.116 = f32[8,1024,1,128]{3,1,2,0:T(8,128)} fusion(f32[8,1024,1,128]{3,1,2,0:T(8,128)} %get-tuple-element.906, s32[]{:T(128)} %get-tuple-element.904, f32[1024,1024]{0,1:T(8,128)S(1)} %get-tuple-element.803, f32[1024]{0:T(1024)S(1)} %get-tuple-element.805, f32[8,1024,1,128]{3,1,2,0:T(8,128)} %get-tuple-element.927, ...), kind=kOutput, calls=%fused_computation.62.clone.1 | convolution fusion | flops 278134784 | bytes 5531136 | tf_op jit(solution)/shard_map/while/body/eval_jaxpr/kqc,ckd->qkd/dot_general | solution.py:65
  257.0 4.0 %fusion.116 = f32[8,1024,1,128]{3,1,2,0:T(8,128)} fusion(f32[8,1024,1,128]{3,1,2,0:T(8,128)} %get-tuple-element.906, s32[]{:T(128)} %get-tuple-element.904, f32[1024,1024]{0,1:T(8,128)S(1)} %get-tuple-element.803, f32[1024]{0:T(1024)S(1)} %get-tuple-element.805, f32[8,1024,1,128]{3,1,2,0:T(8,128)} %get-tuple-element.927, ...), kind=kOutput, calls=%fused_computation.62.clone.1 | convolution fusion | flops 278134784 | bytes 5531136 | tf_op jit(solution)/shard_map/while/body/eval_jaxpr/kqc,ckd->qkd/dot_general | solution.py:65
  264.8 4.0 %fusion.116 = f32[8,1024,1,128]{3,1,2,0:T(8,128)} fusion(f32[8,1024,1,128]{3,1,2,0:T(8,128)} %get-tuple-element.906, s32[]{:T(128)} %get-tuple-element.904, f32[1024,1024]{0,1:T(8,128)S(1)} %get-tuple-element.803, f32[1024]{0:T(1024)S(1)} %get-tuple-element.805, f32[8,1024,1,128]{3,1,2,0:T(8,128)} %get-tuple-element.927, ...), kind=kOutput, calls=%fused_computation.62.clone.1 | convolution fusion | flops 278134784 | bytes 5531136 | tf_op jit(solution)/shard_map/while/body/eval_jaxpr/kqc,ckd->qkd/dot_general | solution.py:65
  272.7 4.0 %fusion.116 = f32[8,1024,1,128]{3,1,2,0:T(8,128)} fusion(f32[8,1024,1,128]{3,1,2,0:T(8,128)} %get-tuple-element.906, s32[]{:T(128)} %get-tuple-element.904, f32[1024,1024]{0,1:T(8,128)S(1)} %get-tuple-element.803, f32[1024]{0:T(1024)S(1)} %get-tuple-element.805, f32[8,1024,1,128]{3,1,2,0:T(8,128)} %get-tuple-element.927, ...), kind=kOutput, calls=%fused_computation.62.clone.1 | convolution fusion | flops 278134784 | bytes 5531136 | tf_op jit(solution)/shard_map/while/body/eval_jaxpr/kqc,ckd->qkd/dot_general | solution.py:65
  280.5 4.0 %fusion.116 = f32[8,1024,1,128]{3,1,2,0:T(8,128)} fusion(f32[8,1024,1,128]{3,1,2,0:T(8,128)} %get-tuple-element.906, s32[]{:T(128)} %get-tuple-element.904, f32[1024,1024]{0,1:T(8,128)S(1)} %get-tuple-element.803, f32[1024]{0:T(1024)S(1)} %get-tuple-element.805, f32[8,1024,1,128]{3,1,2,0:T(8,128)} %get-tuple-element.927, ...), kind=kOutput, calls=%fused_computation.62.clone.1 | convolution fusion | flops 278134784 | bytes 5531136 | tf_op jit(solution)/shard_map/while/body/eval_jaxpr/kqc,ckd->qkd/dot_general | solution.py:65
  288.3 4.0 %fusion.116 = f32[8,1024,1,128]{3,1,2,0:T(8,128)} fusion(f32[8,1024,1,128]{3,1,2,0:T(8,128)} %get-tuple-element.906, s32[]{:T(128)} %get-tuple-element.904, f32[1024,1024]{0,1:T(8,128)S(1)} %get-tuple-element.803, f32[1024]{0:T(1024)S(1)} %get-tuple-element.805, f32[8,1024,1,128]{3,1,2,0:T(8,128)} %get-tuple-element.927, ...), kind=kOutput, calls=%fused_computation.62.clone.1 | convolution fusion | flops 278134784 | bytes 5531136 | tf_op jit(solution)/shard_map/while/body/eval_jaxpr/kqc,ckd->qkd/dot_general | solution.py:65
  296.2 4.0 %fusion.116 = f32[8,1024,1,128]{3,1,2,0:T(8,128)} fusion(f32[8,1024,1,128]{3,1,2,0:T(8,128)} %get-tuple-element.906, s32[]{:T(128)} %get-tuple-element.904, f32[1024,1024]{0,1:T(8,128)S(1)} %get-tuple-element.803, f32[1024]{0:T(1024)S(1)} %get-tuple-element.805, f32[8,1024,1,128]{3,1,2,0:T(8,128)} %get-tuple-element.927, ...), kind=kOutput, calls=%fused_computation.62.clone.1 | convolution fusion | flops 278134784 | bytes 5531136 | tf_op jit(solution)/shard_map/while/body/eval_jaxpr/kqc,ckd->qkd/dot_general | solution.py:65
  304.0 4.0 %fusion.116 = f32[8,1024,1,128]{3,1,2,0:T(8,128)} fusion(f32[8,1024,1,128]{3,1,2,0:T(8,128)} %get-tuple-element.906, s32[]{:T(128)} %get-tuple-element.904, f32[1024,1024]{0,1:T(8,128)S(1)} %get-tuple-element.803, f32[1024]{0:T(1024)S(1)} %get-tuple-element.805, f32[8,1024,1,128]{3,1,2,0:T(8,128)} %get-tuple-element.927, ...), kind=kOutput, calls=%fused_computation.62.clone.1 | convolution fusion | flops 278134784 | bytes 5531136 | tf_op jit(solution)/shard_map/while/body/eval_jaxpr/kqc,ckd->qkd/dot_general | solution.py:65
  316.8 47.4 %all_to_all.64 = bf16[8,128,1024]{2,1,0:T(8,128)(2,1)S(1)} all-to-all(bf16[8,128,1024]{2,1,0:T(8,128)(2,1)} %convert_element_type.37), channel_id=1, replica_groups=mesh['head'=8,'outer'=2,'inner'=16] {'head'}, dimensions={0} | all-to-all | bytes 4194304 | tf_op jit(solution)/shard_map/all_to_all | solution.py:91
  366.6 4.1 %copy.55 = bf16[128,8192]{1,0:T(8,128)(2,1)} copy(bf16[128,8192]{0,1:T(8,128)(2,1)} %bitcast.198) | data formatting | bytes 4194304 | tf_op jit(solution)/shard_map/all_to_all | solution.py:91
  (165 shorter events, 133.2 us)
Async XLA Ops:
  1.8 18.5 %all-to-all-start.1 = ((bf16[128,8,128]{0,2,1:T(8,128)(2,1)}), bf16[128,8,128]{0,2,1:T(8,128)(2,1)S(1)}, u32[]{:S(2)}, u32[]{:S(2)}) async-start(bf16[128,8,128]{0,2,1:T(8,128)(2,1)} %bitcast.2), calls=%async_computation.1 | async-start | bytes 524288 | tf_op jit(solution)/shard_map/all_to_all | solution.py:27
  20.3 16.3 %all-to-all-start.2 = ((bf16[128,8,128]{0,2,1:T(8,128)(2,1)}), bf16[128,8,128]{0,2,1:T(8,128)(2,1)S(1)}, u32[]{:S(2)}, u32[]{:S(2)}) async-start(bf16[128,8,128]{0,2,1:T(8,128)(2,1)} %bitcast.5), calls=%async_computation.2 | async-start | bytes 524288 | tf_op jit(solution)/shard_map/all_to_all | solution.py:28
  27.1 78.3 %copy-start.2 = (s32[32]{0:T(128)S(1)}, s32[32]{0:T(128)}, u32[]{:S(2)}) copy-start(s32[32]{0:T(128)} %param.13) | copy-start | bytes 388
  36.6 88.0 %all-to-all-start = ((bf16[128,8,1024]{2,0,1:T(8,128)(2,1)}), bf16[128,8,1024]{2,0,1:T(8,128)(2,1)S(1)}, u32[]{:S(2)}, u32[]{:S(2)}) async-start(bf16[128,8,1024]{2,0,1:T(8,128)(2,1)} %bitcast.142), calls=%async_computation | async-start | bytes 4194304 | tf_op jit(solution)/shard_map/all_to_all | solution.py:26
  41.5 62.0 %collective-permute-start = (bf16[2,1024,128]{2,1,0:T(8,128)(2,1)}, bf16[2,1024,128]{2,1,0:T(8,128)(2,1)}, u32[]{:S(2)}, u32[]{:S(2)}) collective-permute-start(bf16[2,1024,128]{2,1,0:T(8,128)(2,1)} %pad_maximum_fusion), channel_id=1, source_target_pairs={{0,1},{1,2},{2,3},{3,4},{4,5},{5,6},{6,7},{7,8},{8,9},{9,10},{10,1... | collective-permute-start | bytes 1572872 | tf_op jit(solution)/shard_map/ppermute | solution.py:14
  103.5 20.1 %collective-permute-start.1 = (bf16[2,1024,128]{2,1,0:T(8,128)(2,1)}, bf16[2,1024,128]{2,1,0:T(8,128)(2,1)}, u32[]{:S(2)}, u32[]{:S(2)}) collective-permute-start(bf16[2,1024,128]{2,1,0:T(8,128)(2,1)} %collective-permute-done), channel_id=1, source_target_pairs={{0,1},{1,2},{2,3},{3,4},{4,5},{5,6},{6,7},{7,8},{8,9},{9,10},{10,1... | collective-permute-start | bytes 1572872 | tf_op jit(solution)/shard_map/ppermute | solution.py:14
  181.3 2.3 copy-start
  181.3 2.3 copy-start.1
where the time goes:
time: 372 us; the launch traced here: 371 us
  matrix products  123 us (33%)
  waiting for transfers between devices  93.1 us (25%)
  other arithmetic  56.9 us (15%)
  blocking collectives  47.4 us (13%)
  local copies, waits for them, and re-layouts  29.1 us (8%)
  starting transfers between devices  20 us (5%)
    dot_general x24, matrix products, one_group(): jnp.einsum('kqc,ckd->qkd', weights.astype(jnp.bfloat16), value_heads, pre...  88.2 us
    ppermute x2, waiting for transfers between devices, from_behind(): lax.ppermute(value, axis, [(source, source + steps) for source in range(l...  74.4 us
    reduce_sum x24, other arithmetic, one_group(): new_total = running_total * shrink + jnp.sum(weights, axis=2)  51.9 us
    all_to_all x1, blocking collectives, per_device(): lax.all_to_all(outcome, 'head', split_axis=0, concat_axis=1, tiled=True)  47.4 us
    dot_general x24, matrix products, one_group(): jnp.einsum('qkd,ckd->kqc', query_part, key_heads, preferred_element_type=...  34.6 us
    all_to_all x1, waiting for transfers between devices, per_device(): lax.all_to_all(values, 'head', split_axis=1, concat_axis=0, tiled=True)  9.57 us
    all_to_all x1, waiting for transfers between devices, per_device(): lax.all_to_all(keys, 'head', split_axis=1, concat_axis=0, tiled=True)  9.2 us
    all_to_all x1, starting transfers between devices, per_device(): lax.all_to_all(keys, 'head', split_axis=1, concat_axis=0, tiled=True)  7.57 us
  transfers between devices with their start and end apart: 5, of which 4 were waited for; matrix products, arithmetic and copies ran while one was open for 3% of the time, Pallas kernels for 0%

commit v1 on v0

v1 whole, which is shorter than its diff:
```python
import math

import jax
import jax.numpy as jnp
from jax import lax
from jax.experimental import pallas as pl
from jax.experimental.pallas import tpu as pltpu
from jax.sharding import PartitionSpec as P

D = 128
T = 128
C = 2 * T
KH = 4
GW = 8
W = KH * D
QW = W * GW
BLOCKS = 32
CHIPS = 4 * BLOCKS
NDOCS = 32
MASKED = -1e30
SCALE = 1.4426950408889634 / math.sqrt(D)
MESH = pl.DeviceIdType.MESH

OWN = 0
PREV = {0: 1, 3: 3, 1: 4, 2: 7}
OTHER = {0: 2, 3: 5, 1: 6, 2: 8}


def kernel(
    len_ref, q_ref, k_ref, v_ref, o_ref,
    qbuf, kbuf, vbuf, kfeat, qfeat, top, total, acc, obuf,
    local_sem, out_sem, own_sem, recv_sem, send0, send1, send2, send3, sendx,
    osend, orecv,
):
    head = lax.axis_index("head")
    b = lax.axis_index("outer") * 16 + lax.axis_index("inner")
    zh = head // 2
    c = head % 2

    def device(block, place, core):
        return {
            "head": place * 2 + core,
            "outer": block // 16,
            "inner": block % 16,
        }

    partner = device(b, zh, 1 - c)
    after = lambda core: device((b + 1) % BLOCKS, zh, core)
    before = lambda core: device((b + BLOCKS - 1) % BLOCKS, zh, core)
    beside = lambda dz, core: device(b, (zh + dz) % 4, core)

    def rows(core):
        return pl.ds(pl.multiple_of(core * T, T), T)

    def cols(core, width):
        return pl.ds(pl.multiple_of(core * width, width), width)

    @pl.when(b < 2)
    def _():
        def clear(i, carry):
            kbuf[i + 1] = jnp.zeros((C, W), jnp.bfloat16)
            vbuf[i + 1] = jnp.zeros((C, W), jnp.bfloat16)
            return carry

        lax.fori_loop(0, 8, clear, 0)

    local = [
        pltpu.make_async_copy(k_ref.at[:, cols(c, W)], kbuf.at[OWN, rows(c), :], local_sem.at[0]),
        pltpu.make_async_copy(v_ref.at[:, cols(c, W)], vbuf.at[OWN, rows(c), :], local_sem.at[1]),
        pltpu.make_async_copy(q_ref.at[:, cols(c, QW)], qbuf.at[rows(c), :], local_sem.at[2]),
    ]
    for copy in local:
        copy.start()

    barrier = pltpu.get_barrier_semaphore()
    greeted = [partner, after(0), after(1), before(0), before(1)]
    greeted += [beside(dz, core) for dz in (1, 2, 3) for core in (c, 1 - c)]
    for target in greeted:
        pl.semaphore_signal(barrier, inc=1, device_id=target, device_id_type=MESH)

    pl.semaphore_wait(barrier, len(greeted))

    def send(src, dst, send_sem, recv, target):
        return pltpu.make_async_remote_copy(
            src_ref=src, dst_ref=dst, send_sem=send_sem, recv_sem=recv,
            device_id=target, device_id_type=MESH,
        )

    bufs = (kbuf, vbuf)
    inputs = (k_ref, v_ref)

    first = []
    for i in range(2):
        core = (c + i) % 2
        for kv in range(2):
            first.append(
                send(
                    inputs[kv].at[:, cols(core, W)],
                    bufs[kv].at[PREV[0], rows(c), :],
                    send1.at[i, kv],
                    recv_sem.at[PREV[0], c, kv],
                    after(core),
                )
            )
    own = [
        send(
            inputs[kv].at[:, cols(1 - c, W)],
            bufs[kv].at[OWN, rows(c), :],
            send0.at[kv],
            own_sem.at[kv],
            partner,
        )
        for kv in range(2)
    ]
    own.append(
        send(q_ref.at[:, cols(1 - c, QW)], qbuf.at[rows(c), :], send0.at[2], own_sem.at[2], partner)
    )
    last = []
    for dz in (1, 2, 3):
        for i in range(2):
            core = (c + i) % 2
            for kv in range(2):
                last.append(
                    (
                        dz,
                        send(
                            inputs[kv].at[:, cols(core, W)],
                            bufs[kv].at[OTHER[4 - dz], rows(c), :],
                            sendx.at[dz - 1, i, kv],
                            recv_sem.at[OTHER[4 - dz], c, kv],
                            beside(dz, core),
                        ),
                    )
                )

    @pl.when(b < BLOCKS - 1)
    def _():
        for copy in first:
            copy.start()

    for copy in own:
        copy.start()

    for dz in (1, 2, 3):

        @pl.when((b == BLOCKS - 1) & (zh + dz < 4))
        def _():
            for place, copy in last:
                if place == dz:
                    copy.start()

    lane = lax.broadcasted_iota(jnp.int32, (1, 128), 1)
    begins = jnp.zeros((1, 128), jnp.int32)
    ends = jnp.zeros((1, 128), jnp.int32)
    end = jnp.int32(0)
    for j in range(NDOCS):
        begins = jnp.where(lane == j, end, begins)
        end = end + len_ref[j]
        ends = jnp.where(lane == j, end, ends)

    row_in_piece = lax.broadcasted_iota(jnp.int32, (C, 128), 0)

    def inside(chip):
        position = row_in_piece + (chip % CHIPS) * C
        return (position >= begins) & (position < ends)

    here = 4 * b + zh
    qfeat[...] = jnp.where(inside(here), 0.0, MASKED).astype(jnp.bfloat16)
    kfeat[OWN] = jnp.where(inside(here), 1.0, 0.0).astype(jnp.bfloat16)
    for r in range(4):
        chip = 4 * (b + BLOCKS - 1) + (zh + r) % 4
        kfeat[PREV[r]] = jnp.where(inside(chip), 1.0, 0.0).astype(jnp.bfloat16)
        chip = 4 * (b + BLOCKS - 2) + zh + r + 4 * ((zh + r) // 4)
        kfeat[OTHER[r]] = jnp.where(inside(chip), 1.0, 0.0).astype(jnp.bfloat16)

    ones = jnp.ones((C, D), jnp.bfloat16)

    def scores_of(slot, g):
        features = qfeat[...]
        queries = jnp.concatenate(
            [
                jnp.concatenate(
                    [qbuf[:, pl.ds(pl.multiple_of(g * GW * D, D) + j * D, D)], features], axis=1
                )
                for j in range(GW)
            ],
            axis=0,
        )
        keys = jnp.concatenate(
            [kbuf[slot, :, pl.ds(pl.multiple_of(g * D, D), D)], kfeat[slot]], axis=1
        )
        return lax.dot_general(
            queries, keys, (((1,), (1,)), ((), ())), preferred_element_type=jnp.float32
        )

    def summed(weights, slot, g):
        held = jnp.concatenate([vbuf[slot, :, pl.ds(pl.multiple_of(g * D, D), D)], ones], axis=1)
        return jnp.dot(weights.astype(jnp.bfloat16), held, preferred_element_type=jnp.float32)

    def attend_own(g, carry):
        scores = scores_of(OWN, g)
        key_at = lax.broadcasted_iota(jnp.int32, (GW * C, C), 1)
        query_at = lax.broadcasted_iota(jnp.int32, (GW * C, C), 0) & (C - 1)
        scores = jnp.where(key_at <= query_at, scores, MASKED)
        new_top = jnp.max(scores, axis=1, keepdims=True)
        both = summed(jnp.exp2((scores - new_top) * SCALE), OWN, g)
        top[g] = jnp.broadcast_to(new_top, (GW * C, D))
        acc[g] = both[:, :D]
        total[g] = both[:, D:]
        return carry

    def attend(slot, g):
        scores = scores_of(slot, g)
        old_top = top[g]
        new_top = jnp.maximum(old_top, jnp.max(scores, axis=1, keepdims=True))
        both = summed(jnp.exp2((scores - new_top[:, :1]) * SCALE), slot, g)
        shrink = jnp.exp2((old_top - new_top) * SCALE)
        top[g] = new_top
        acc[g] = acc[g] * shrink + both[:, :D]
        total[g] = total[g] * shrink + both[:, D:]

    def arrival(slot, sub, kv):
        part = bufs[kv].at[slot, rows(sub), :]
        return send(part, part, send0.at[0], recv_sem.at[slot, sub, kv], partner)

    def beside_send(slot, there, sub, kv, dz, index):
        return send(
            bufs[kv].at[slot, rows(sub), :],
            bufs[kv].at[there, rows(sub), :],
            send2.at[index, sub, kv],
            recv_sem.at[there, sub, kv],
            beside(dz, c),
        )

    def onward(r, sub, kv):
        forth = 1 - 2 * ((zh + r) // 4)
        return send(
            bufs[kv].at[PREV[r], rows(sub), :],
            bufs[kv].at[OTHER[r], rows(sub), :],
            send3.at[r, sub, kv],
            recv_sem.at[OTHER[r], sub, kv],
            device((b + BLOCKS + forth) % BLOCKS, zh, c),
        )

    def goes_onward(r):
        back = zh + r >= 4
        if r == 0:
            return (b > 0) & (b < BLOCKS - 1)
        return (b > 0) & (back | ((b < BLOCKS - 1) & (b != 15)))

    def start_onward(r, sub):
        @pl.when(goes_onward(r))
        def _():
            for kv in range(2):
                onward(r, sub, kv).start()

    def take_first(sub):
        @pl.when(b > 0)
        def _():
            for kv in range(2):
                arrival(PREV[0], sub, kv).wait_recv()
                beside_send(PREV[0], PREV[3], sub, kv, 1, 0).start()
                beside_send(PREV[0], PREV[1], sub, kv, 3, 1).start()

        start_onward(0, sub)

    def right_relay(kv):
        return send(
            bufs[kv].at[PREV[3], pl.ds(0, T), :],
            bufs[kv].at[PREV[2], pl.ds(0, T), :],
            send2.at[2, 0, kv],
            recv_sem.at[PREV[2], 0, kv],
            beside(1, c),
        )

    def left_relay(kv):
        return send(
            bufs[kv].at[PREV[1], pl.ds(T, T), :],
            bufs[kv].at[PREV[2], pl.ds(T, T), :],
            send2.at[2, 1, kv],
            recv_sem.at[PREV[2], 1, kv],
            beside(3, c),
        )

    def take_beside(sub):
        @pl.when(b > 0)
        def _():
            for kv in range(2):
                arrival(PREV[3], sub, kv).wait_recv()
                arrival(PREV[1], sub, kv).wait_recv()

            @pl.when(sub == 0)
            def _():
                for kv in range(2):
                    right_relay(kv).start()

            @pl.when(sub == 1)
            def _():
                for kv in range(2):
                    left_relay(kv).start()

        start_onward(3, sub)
        start_onward(1, sub)

    def take_relayed():
        @pl.when(b > 0)
        def _():
            for sub in range(2):
                for kv in range(2):
                    arrival(PREV[2], sub, kv).wait_recv()

        for sub in range(2):
            start_onward(2, sub)

    def across(dz, sub, kv):
        return send(
            bufs[kv].at[OTHER[0], rows(sub), :],
            bufs[kv].at[OTHER[4 - dz], rows(sub), :],
            sendx.at[dz - 1, sub, kv],
            recv_sem.at[OTHER[4 - dz], sub, kv],
            beside(dz, c),
        )

    def take_other(r):
        @pl.when((zh + r >= 4) | (b >= 2))
        def _():
            for sub in range(2):
                for kv in range(2):
                    arrival(OTHER[r], sub, kv).wait_recv()

        if r == 0:
            for dz in (1, 2, 3):

                @pl.when((b == 16) & (zh + dz >= 4))
                def _():
                    for sub in range(2):
                        for kv in range(2):
                            across(dz, sub, kv).start()

    for copy in local:
        copy.wait()
    for copy in own:
        copy.wait_recv()

    lax.fori_loop(0, KH, attend_own, 0)
    take_first(c)
    take_first(1 - c)

    def take_sixth():
        take_relayed()
        take_other(1)

    schedule = {
        (2, 0): lambda: take_other(0),
        (2, 2): lambda: take_beside(c),
        (3, 0): lambda: take_beside(1 - c),
        (5, 0): lambda: take_other(3),
        (6, 0): lambda: take_sixth(),
        (8, 0): lambda: take_other(2),
    }

    def step(t, carry):
        for (slot, g), action in schedule.items():
            pl.when(t == slot * KH + g)(action)
        attend(t // KH, t % KH)
        return carry

    lax.fori_loop(KH, 9 * KH, step, 0)

    outgoing = []
    for g in range(KH):
        outcome = (acc[g] / total[g]).astype(jnp.bfloat16)
        for j in range(GW):
            obuf[:, pl.ds((g * GW + j) * D, D)] = outcome[j * C : (j + 1) * C]
        part = pl.ds(g * GW * D, GW * D)
        place = pl.ds(pl.multiple_of(c * QW, QW) + g * GW * D, GW * D)
        kept = pltpu.make_async_copy(obuf.at[rows(c), part], o_ref.at[:, place], out_sem.at[g])
        given = send(
            obuf.at[rows(1 - c), part], o_ref.at[:, place], osend.at[g], orecv.at[g], partner
        )
        given.start()
        kept.start()
        outgoing.append((kept, given))

    for kept, given in outgoing:
        kept.wait()
        given.wait()
    for copy in own:
        copy.wait_send()

    @pl.when(b < BLOCKS - 1)
    def _():
        for copy in first:
            copy.wait_send()

    for dz in (1, 2, 3):

        @pl.when((b == BLOCKS - 1) & (zh + dz < 4))
        def _():
            for place, copy in last:
                if place == dz:
                    copy.wait_send()

        @pl.when((b == 16) & (zh + dz >= 4))
        def _():
            for sub in range(2):
                for kv in range(2):
                    across(dz, sub, kv).wait_send()

    @pl.when(b > 0)
    def _():
        for kv in range(2):
            for sub in range(2):
                beside_send(PREV[0], PREV[3], sub, kv, 1, 0).wait_send()
                beside_send(PREV[0], PREV[1], sub, kv, 3, 1).wait_send()
            right_relay(kv).wait_send()
            left_relay(kv).wait_send()

    for r in range(4):

        @pl.when(goes_onward(r))
        def _():
            for sub in range(2):
                for kv in range(2):
                    onward(r, sub, kv).wait_send()


def per_device(query, keys, values, lengths):
    any_space = pl.BlockSpec(memory_space=pl.ANY)
    dma = pltpu.SemaphoreType.DMA
    return pl.pallas_call(
        kernel,
        out_shape=jax.ShapeDtypeStruct(query.shape, jnp.bfloat16),
        in_specs=[pl.BlockSpec(memory_space=pltpu.SMEM), any_space, any_space, any_space],
        out_specs=any_space,
        scratch_shapes=[
            pltpu.VMEM((C, QW), jnp.bfloat16),
            pltpu.VMEM((9, C, W), jnp.bfloat16),
            pltpu.VMEM((9, C, W), jnp.bfloat16),
            pltpu.VMEM((9, C, 128), jnp.bfloat16),
            pltpu.VMEM((C, 128), jnp.bfloat16),
            pltpu.VMEM((KH, GW * C, D), jnp.float32),
            pltpu.VMEM((KH, GW * C, D), jnp.float32),
            pltpu.VMEM((KH, GW * C, D), jnp.float32),
            pltpu.VMEM((C, QW), jnp.bfloat16),
            dma((3,)),
            dma((KH,)),
            dma((3,)),
            dma((9, 2, 2)),
            dma((3,)),
            dma((2, 2)),
            dma((3, 2, 2)),
            dma((4, 2, 2)),
            dma((3, 2, 2)),
            dma((KH,)),
            dma((KH,)),
        ],
        compiler_params=pltpu.CompilerParams(
            collective_id=0, has_side_effects=True, vmem_limit_bytes=58 * 1024 * 1024
        ),
        name="attend_pack",
    )(lengths, query, keys, values)


def solution(mesh):
    placed = P(("outer", "inner", "head"), None)
    return jax.shard_map(
        per_device,
        mesh=mesh,
        in_specs=(placed, placed, placed, P()),
        out_specs=placed,
        check_vma=False,
    )
```

time: 372 us -> 168 us (0.45)
  the two profiles are of different devices: /device:TPU:32 before, /device:TPU:159 now
where the time goes in v1:
time: 168 us
  Pallas kernels  165 us (98%)
  local copies, waits for them, and re-layouts  3.1 us (2%)
    pallas_call x1, Pallas kernels, per_device(): pl.pallas_call(kernel, out_shape=jax.ShapeDtypeStruct(query.shape, jnp.bf...  165 us

profile of v1, /device:TPU:159, one launch (start us, length us, event | category | flops | bytes accessed | tf_op | source)
XLA Modules:
  0.0 167.7 jit_solution(4338504056550519982)
XLA Ops:
  0.0 164.6 %attend_pack.1 = bf16[128,8192]{1,0:T(8,128)(2,1)} custom-call(s32[32]{0:T(128)} %len_ref.1, bf16[128,8192]{1,0:T(8,128)(2,1)} %q_ref.1, bf16[128,1024]{1,0:T(8,128)(2,1)} %k_ref.1, bf16[128,1024]{1,0:T(8,128)(2,1)} %v_ref.1), custom_call_target="tpu_custom_call" | custom-call | tf_op jit(solution)/shard_map/attend_pack/pallas_call | solution.py:431
  164.6 3.1 %copy.6 = bf16[128,8192]{1,0:T(8,128)(2,1)} copy(bf16[128,8192]{1,0:T(8,128)(2,1)} %attend_pack.1) | data formatting | bytes 4194304
